TPU v7x, 32 devices: a whole 2x2x4 slice. The times are simulated.
32 devices in a mesh: dp: 4 (over x, core), seq: 8 (over z, y).
Axes of the slice: x: 2, y: 2, z: 4, core: 2. Of those that a mesh axis runs over, the one named last changes fastest.
Arguments:
- tokens: bfloat16 [8, 1152, 1280], P('dp', 'seq'), may hold values from -60 to 60
- pre_gain: float32 [1280], replicated, may hold values from 0.5 to 1.5
- pre_shift: float32 [1280], replicated, may hold values from -3 to 3
- w_qkv: bfloat16 [1280, 3840], P('dp'), may hold values from -4 to 4
- qkv_bias: float32 [3840], replicated, may hold values from -3 to 3
- w_out: bfloat16 [1280, 1280], P('dp'), may hold values from -0.15625 to 0.15625
- out_bias: float32 [1280], replicated, may hold values from -3 to 3
- mlp_gain: float32 [1280], replicated, may hold values from 0.5 to 1.5
- mlp_shift: float32 [1280], replicated, may hold values from -3 to 3
- w_up: bfloat16 [1280, 2560], P('dp'), may hold values from -0.15625 to 0.15625
- up_bias: float32 [2560], replicated, may hold values from -3 to 3
- w_down: bfloat16 [2560, 1280], P('dp'), may hold values from -0.125 to 0.125
- down_bias: float32 [1280], replicated, may hold values from -3 to 3
Outputs:
- layer_out: bfloat16 [8, 1152, 1280], P('dp', 'seq')
All inputs are finite; a program needn't handle non-finite values.
Results may differ from a plain program's by a relative error of at most 0.0039.
Values may be sent and summed in bfloat16 or wider, within the bound.
A program may use at most 128 MiB of HBM per device.

v0:
```python
import functools
import math

import jax
import jax.numpy as jnp
from jax import lax
from jax.experimental import pallas as pl
from jax.experimental.pallas import tpu as pltpu
from jax.sharding import PartitionSpec as P

HEADS = 16
HEAD_DIM = 80
LANES = 128
EPSILON = 1e-05
MESH = pl.DeviceIdType.MESH
VMEM = pl.BlockSpec(memory_space=pltpu.VMEM)


def normalize(features, gain, shift):
    average = jnp.mean(features, axis=-1, keepdims=True)
    centered = features - average
    spread = jnp.mean(centered * centered, axis=-1, keepdims=True)
    return centered * lax.rsqrt(spread + EPSILON) * gain + shift


def fold_rows(left_side, shard_piece):
    return jnp.dot(left_side, shard_piece, preferred_element_type=jnp.float32)


def ring_to_seq(place, n):
    back = place // (n // 2)
    return (1 - back) * 2 * place + back * (2 * (n - 1 - place) + 1)


def seq_to_ring(s, n):
    odd = s % 2
    return (1 - odd) * (s // 2) + odd * (n - 1 - s // 2)


def layer_kernel(
    n,
    n_dp,
    heads,
    head_size,
    block_rows,
    x_ref,
    w_ref,
    b_ref,
    out_shard,
    up_shard,
    down_shard,
    tok_ref,
    ob_ref,
    gain_ref,
    shift_ref,
    ub_ref,
    middle_ref,
    hidden_ref,
    down_full,
    out_full,
    up_full,
    ctx_ref,
    buf,
    wraw,
    wbuf,
    packed,
    mixed,
    landed,
    tok_send,
    tok_recv,
    w_send,
    w_recv,
    f_send,
    f_recv,
    own_sem,
    c_send,
    c_recv,
):
    d, s = lax.axis_index("dp"), lax.axis_index("seq")
    place = seq_to_ring(s, n)
    right = ring_to_seq((place + 1) % n, n)
    left = ring_to_seq((place + n - 1) % n, n)
    sibling = d + 1 - 2 * (d % 2)
    half = x_ref.shape[0] // 2
    images, length, _ = packed.shape
    tok = length // n
    steps = n // 2
    pairs = n_dp // 2
    span = heads * head_size
    shards_of = (w_ref, out_shard, up_shard, down_shard)
    wholes = (wraw, out_full, up_full, down_full)
    factor = math.log2(math.e) / math.sqrt(head_size)

    barrier = pltpu.get_barrier_semaphore()
    for t in range(1, n):
        pl.semaphore_signal(barrier, inc=1, device_id=(d, (s + t) % n), device_id_type=MESH)
    for j in range(1, pairs):
        pl.semaphore_signal(barrier, inc=1, device_id=((d + 2 * j) % n_dp, s), device_id_type=MESH)
    pl.semaphore_signal(barrier, inc=1, device_id=(sibling, s), device_id_type=MESH)
    pl.semaphore_wait(barrier, n - 1 + pairs)

    def token_copy(way, t, h, arriving=False):
        back = t + 1 if arriving else t
        origin = (place + n - back) % n if way == 0 else (place + back) % n
        part = pl.ds(h * half, half)
        here = buf.at[origin, part]
        return pltpu.make_async_remote_copy(
            src_ref=x_ref.at[part] if (t == 0 and not arriving) else here,
            dst_ref=here,
            send_sem=tok_send.at[way, t, h],
            recv_sem=tok_recv.at[way, t, h],
            device_id=(d, right if way == 0 else left),
            device_id_type=MESH,
        )

    def slab(k, owner):
        depth = shards_of[k].shape[0]
        return pl.ds(pl.multiple_of(owner * depth, 16), depth)

    def w_copy(k, j, arriving=False):
        owner = (d + n_dp - 2 * j) % n_dp if arriving else d
        return pltpu.make_async_remote_copy(
            src_ref=shards_of[k],
            dst_ref=wholes[k].at[slab(k, owner)],
            send_sem=w_send.at[k, j],
            recv_sem=w_recv.at[k, j],
            device_id=((d + 2 * j) % n_dp, s),
            device_id_type=MESH,
        )

    def f_copy(k, j, arriving=False):
        base = sibling if arriving else d
        owner = (base + n_dp - 2 * j) % n_dp
        there = wholes[k].at[slab(k, owner)]
        return pltpu.make_async_remote_copy(
            src_ref=shards_of[k] if j == 0 else there,
            dst_ref=there,
            send_sem=f_send.at[k, j],
            recv_sem=f_recv.at[k, j],
            device_id=(sibling, s),
            device_id_type=MESH,
        )

    def pass_on(k):
        for j in range(1, pairs):
            w_copy(k, j, True).wait_recv()
            f_copy(k, j).start()

    def own_copy(k):
        return pltpu.make_async_copy(shards_of[k], wholes[k].at[slab(k, d)], own_sem.at[k])

    def rows_of(owner):
        return pl.ds(pl.multiple_of(owner * tok, 16), tok)

    def ctx_copy(i, t, arriving=False):
        peer = (s + t) % n
        slot = (s + n - t) % n if arriving else s
        return pltpu.make_async_remote_copy(
            src_ref=mixed.at[i, rows_of(peer), :],
            dst_ref=landed.at[slot, i],
            send_sem=c_send.at[i, t],
            recv_sem=c_recv.at[i, t],
            device_id=(d, peer),
            device_id_type=MESH,
        )

    for j in range(1, pairs):
        w_copy(0, j).start()
    f_copy(0, 0).start()
    for h in range(2):
        for way in range(2):
            token_copy(way, 0, h).start()
    for k in range(1, 4):
        for j in range(1, pairs):
            w_copy(k, j).start()
        f_copy(k, 0).start()
    own_copy(3).start()
    for k in range(3):
        wholes[k][slab(k, d), :] = shards_of[k][...]

    def process(block, owner):
        y = jnp.dot(block, wbuf[...], preferred_element_type=jnp.float32) + b_ref[...]
        y = y.astype(jnp.bfloat16)
        for i in range(images):
            packed[i, rows_of(owner), :] = y[i * tok : (i + 1) * tok]

    for t in range(steps):
        last = t == steps - 1
        for h in range(2):
            for way in range(2):
                if last and h != way:
                    continue
                token_copy(way, t, h, True).wait_recv()
                if t < steps - 2 or (t == steps - 2 and h == way):
                    token_copy(way, t + 1, h).start()
        if t == 0:
            pass_on(0)
            for j in range(pairs):
                f_copy(0, j, True).wait_recv()
            wbuf[...] = jnp.zeros_like(wbuf)
            for g in range(3 * heads):
                wbuf[:, g * LANES : g * LANES + head_size] = wraw[:, g * head_size : (g + 1) * head_size]
            process(x_ref[...], s)
        if last:
            pass_on(1)
            far = (place + n // 2) % n
            process(buf[far], ring_to_seq(far, n))
        else:

            def both(i, carry):
                origin = (place + n - (t + 1) + i * 2 * (t + 1)) % n
                process(buf[origin], ring_to_seq(origin, n))
                return carry

            lax.fori_loop(0, 2, both, 0)

    def attend_image(i, carry):
        def attend_block(block, inner):
            at = pl.ds(pl.multiple_of(block * block_rows, 16), block_rows)
            parts = []
            for h in range(heads):
                base = h * 3 * LANES
                queries = packed[i, at, base : base + LANES]
                key_rows = packed[i, :, base + LANES : base + 2 * LANES]
                value_rows = packed[i, :, base + 2 * LANES : base + 3 * LANES]
                scores = lax.dot_general(
                    queries, key_rows, (((1,), (1,)), ((), ())), preferred_element_type=jnp.float32
                )
                highest = jnp.max(scores, axis=-1, keepdims=True)
                weights = jnp.exp2((scores - highest) * factor).astype(jnp.bfloat16)
                summed = jnp.dot(weights, value_rows, preferred_element_type=jnp.float32)
                parts.append(summed[:, :head_size] / summed[:, head_size : head_size + 1])
            mixed[i, at, :] = jnp.concatenate(parts, axis=-1).astype(jnp.bfloat16)
            return inner

        lax.fori_loop(0, length // block_rows, attend_block, 0)
        landed[s, i] = mixed[i, rows_of(s), :]
        for t in range(1, n):
            ctx_copy(i, t).start()
        return carry

    lax.fori_loop(0, images, attend_image, 0)
    pass_on(2)

    def gather_image(i, carry):
        for t in range(1, n):
            ctx_copy(i, t, True).wait_recv()
        rows = pl.ds(pl.multiple_of(i * tok, 16), tok)
        for owner in range(n):
            ctx_ref[rows, owner * span : (owner + 1) * span] = landed[owner, i]
        return carry

    for k in range(1, 3):
        for j in range(pairs):
            f_copy(k, j, True).wait_recv()
    lax.fori_loop(0, images, gather_image, 0)

    def tile_of(c):
        return pl.ds(pl.multiple_of(c * 2 * LANES, 2 * LANES), 2 * LANES)

    def out_tile(c, carry):
        cols = tile_of(c)
        attended = jnp.dot(ctx_ref[...], out_full[:, cols], preferred_element_type=jnp.float32)
        middle_ref[:, cols] = tok_ref[:, cols].astype(jnp.float32) + attended + ob_ref[:, cols]
        return carry

    def up_tile(c, carry):
        cols = tile_of(c)
        lifted = jnp.dot(ctx_ref[...], up_full[:, cols], preferred_element_type=jnp.float32)
        lifted = lifted + ub_ref[:, cols]
        hidden = 0.5 * lifted * (1.0 + lax.erf(lifted * math.sqrt(0.5)))
        hidden_ref[:, cols] = hidden.astype(jnp.bfloat16)
        return carry

    lax.fori_loop(0, out_full.shape[1] // (2 * LANES), out_tile, 0)
    ctx_ref[...] = normalize(middle_ref[...], gain_ref[...], shift_ref[...]).astype(jnp.bfloat16)
    lax.fori_loop(0, up_full.shape[1] // (2 * LANES), up_tile, 0)
    pass_on(3)

    for k in range(4):
        for j in range(pairs):
            if k == 3:
                f_copy(k, j, True).wait_recv()
            if j > 0:
                w_copy(k, j).wait_send()
            f_copy(k, j).wait_send()
    own_copy(3).wait()
    for t in range(steps):
        for h in range(2):
            for way in range(2):
                if t < steps - 1 or h == way:
                    token_copy(way, t, h).wait_send()
    for i in range(images):
        for t in range(1, n):
            ctx_copy(i, t).wait_send()


def layer_until_hidden(
    normed, w_cols, bias, w_out, w_up, w_down, tokens, out_bias, gain, shift, up_bias, images, heads, n, n_dp
):
    rows, width = normed.shape
    columns = 3 * heads * LANES
    tok = rows // images
    length = n * tok
    pairs = n_dp // 2
    span = heads * HEAD_DIM
    block_rows = max(r for r in range(16, 385, 16) if length % r == 0)
    dma = pltpu.SemaphoreType.DMA
    half = jnp.bfloat16
    anywhere = pl.BlockSpec(memory_space=pl.ANY)

    def full(shard):
        return (n_dp * shard.shape[0], shard.shape[1])

    return pl.pallas_call(
        functools.partial(layer_kernel, n, n_dp, heads, HEAD_DIM, block_rows),
        out_shape=(
            jax.ShapeDtypeStruct((rows, width), jnp.float32),
            jax.ShapeDtypeStruct((rows, w_up.shape[1]), half),
            jax.ShapeDtypeStruct(full(w_down), half),
        ),
        in_specs=[VMEM] * 11,
        out_specs=(VMEM, VMEM, anywhere),
        scratch_shapes=[
            pltpu.VMEM(full(w_out), half),
            pltpu.VMEM(full(w_up), half),
            pltpu.VMEM((rows, n * span), half),
            pltpu.VMEM((n, rows, width), half),
            pltpu.VMEM(full(w_cols), half),
            pltpu.VMEM((width, columns), half),
            pltpu.VMEM((images, length, columns), half),
            pltpu.VMEM((images, length, span), half),
            pltpu.VMEM((n, images, tok, span), half),
            dma((2, n // 2, 2)),
            dma((2, n // 2, 2)),
            dma((4, pairs)),
            dma((4, pairs)),
            dma((4, pairs)),
            dma((4, pairs)),
            dma((4,)),
            dma((images, n)),
            dma((images, n)),
        ],
        compiler_params=pltpu.CompilerParams(
            collective_id=0, has_side_effects=True, vmem_limit_bytes=56 * 1024 * 1024
        ),
        name="layer_until_hidden",
    )(normed, w_cols, bias, w_out, w_up, w_down, tokens, out_bias, gain, shift, up_bias)


def head_columns(array, s, heads, head_size):
    span = heads * 3 * head_size
    mine = lax.dynamic_slice_in_dim(array, s * span, span, axis=1)
    mine = mine.reshape(array.shape[0], heads, 3, head_size)
    return jnp.pad(mine, ((0, 0), (0, 0), (0, 0), (0, LANES - head_size)))


def shards(
    n,
    n_dp,
    tokens,
    pre_gain,
    pre_shift,
    w_qkv,
    qkv_bias,
    w_out,
    out_bias,
    mlp_gain,
    mlp_shift,
    w_up,
    up_bias,
    w_down,
    down_bias,
):
    images_here, tok_here, width = tokens.shape
    row_count = images_here * tok_here
    heads_here = HEADS // n
    columns = heads_here * 3 * LANES
    s = lax.axis_index("seq")
    residual = tokens.reshape(row_count, width).astype(jnp.float32)
    normed = normalize(residual, pre_gain, pre_shift).astype(jnp.bfloat16)
    span = heads_here * 3 * HEAD_DIM
    w_cols = lax.dynamic_slice_in_dim(w_qkv, s * span, span, axis=1)
    bias = head_columns(qkv_bias[None], s, heads_here, HEAD_DIM)
    bias = bias.at[:, :, 2, HEAD_DIM].set(1.0).reshape(1, columns)
    middle, hidden, w_down = layer_until_hidden(
        normed,
        w_cols,
        bias,
        w_out,
        w_up,
        w_down,
        tokens.reshape(row_count, width),
        out_bias[None],
        mlp_gain[None],
        mlp_shift[None],
        up_bias[None],
        images_here,
        heads_here,
        n,
        n_dp,
    )
    lowered = fold_rows(hidden, w_down)
    result = (middle + lowered + down_bias).astype(jnp.bfloat16)
    return result.reshape(images_here, tok_here, width)


def solution(mesh):
    in_specs = (
        P("dp", "seq", None),
        P(),
        P(),
        P("dp", None),
        P(),
        P("dp", None),
        P(),
        P(),
        P(),
        P("dp", None),
        P(),
        P("dp", None),
        P(),
    )
    out_specs = P("dp", "seq", None)
    step = functools.partial(shards, mesh.shape["seq"], mesh.shape["dp"])
    return jax.shard_map(step, mesh=mesh, in_specs=in_specs, out_specs=out_specs, check_vma=False)
```

profile of v0, /device:TPU:1, one launch (start us, length us, event | category | flops | bytes accessed | tf_op | source)
XLA Modules:
  0.0 127.5 jit_solution(6858103235232972324)
XLA Ops:
  0.0 0.0 copy-start
  0.0 0.0 copy-start.1
  0.0 0.0 copy-start.2
  0.0 0.0 copy-start.7
  0.0 0.0 copy-start.6
  0.0 0.0 copy-start.5
  0.0 0.0 copy-start.3
  0.1 0.0 copy-start.4
  0.1 0.9 dynamic-slice.11
  1.0 0.1 reshape.88
  1.1 0.2 scatter.4
  1.3 0.6 reshape.89.b_ref
  1.9 1.3 %convert_reduce_fusion = f32[2,144]{1,0:T(2,128)S(1)} fusion(bf16[2,144,1280]{2,1,0:T(8,128)(2,1)} %param.15), kind=kLoop, calls=%fused_computation.4 | loop fusion | flops 736992 | bytes 738432 | tf_op jit(solution)/shard_map/reduce_sum | solution.py:20
  3.2 1.5 %fusion.3 = f32[2,144]{1,0:T(2,128)S(1)} fusion(bf16[2,144,1280]{2,1,0:T(8,128)(2,1)} %param.15, f32[2,144]{1,0:T(2,128)S(1)} %broadcast_multiply_fusion), kind=kLoop, calls=%fused_computation.6 | loop fusion | flops 1474272 | bytes 739584 | tf_op jit(solution)/shard_map/reduce_sum | solution.py:22
  4.7 0.1 div.9
  4.7 0.1 rsqrt.12
  4.8 0.0 copy-done.5
  4.8 0.6 broadcast_in_dim.8.ob_ref
  5.4 0.0 copy-done.6
  5.4 0.6 broadcast_in_dim.9.gain_ref
  6.0 0.0 copy-done.7
  6.0 0.6 broadcast_in_dim.20.shift_ref
  6.6 0.0 copy-done.2
  6.6 0.6 broadcast_in_dim.21.ub_ref
  7.2 0.0 copy-done
  7.2 0.9 constant_dynamic-slice_fusion.w_ref
  8.1 0.0 copy-done.1
  8.1 0.0 copy-done.3
  8.1 0.0 copy-done.4
  8.2 1.2 add_convert_fusion.x_ref
  9.4 0.0 copy-start.8
  9.4 111.5 %layer_until_hidden.1 = (f32[288,1280]{1,0:T(8,128)}, bf16[288,2560]{1,0:T(8,128)(2,1)}, bf16[2560,1280]{1,0:T(8,128)(2,1)}) custom-call(bf16[288,1280]{1,0:T(8,128)(2,1)} %add_convert_fusion.x_ref, bf16[320,480]{1,0:T(8,128)(2,1)} %constant_dynamic-slice_fusion.w_ref, f32[1,768]{1,0:T(1,128)} %reshape.89.b_ref, bf16[320,1280]{1,0:T(8,128)(2,1)} %out_shard.1, ...), custom_call_target="tpu_custom_call" | custom-call | tf_op jit(solution)/shard_map/layer_until_hidden/pallas_call | solution.py:315
  120.9 0.0 copy-done.8
  120.9 6.6 %fusion.1 = bf16[288,1280]{1,0:T(8,128)(2,1)} fusion(f32[288,1280]{1,0:T(8,128)} %get-tuple-element.20, bf16[288,2560]{1,0:T(8,128)(2,1)} %get-tuple-element.21, bf16[2560,1280]{1,0:T(8,128)(2,1)} %get-tuple-element.22, f32[1280]{0:T(1024)S(1)} %copy-done.8), kind=kOutput, calls=%fused_computation.2 | convolution fusion | flops 1888542720 | bytes 10245120 | tf_op jit(solution)/shard_map/dot_general | solution.py:27
  (4 shorter events, 0.0 us)
Async XLA Ops:
  0.0 7.2 %copy-start = (bf16[320,3840]{1,0:T(8,128)(2,1)S(1)}, bf16[320,3840]{1,0:T(8,128)(2,1)}, u32[]{:S(2)}) copy-start(bf16[320,3840]{1,0:T(8,128)(2,1)} %param.18) | copy-start | bytes 7372804
  0.0 8.1 %copy-start.1 = (bf16[2,144,1280]{2,1,0:T(8,128)(2,1)S(1)}, bf16[2,144,1280]{2,1,0:T(8,128)(2,1)}, u32[]{:S(2)}) copy-start(bf16[2,144,1280]{2,1,0:T(8,128)(2,1)} %param.15) | copy-start | bytes 2211844
  0.0 6.6 %copy-start.2 = (f32[2560]{0:T(1024)S(1)}, f32[2560]{0:T(1024)}, u32[]{:S(2)}) copy-start(f32[2560]{0:T(1024)} %param.25) | copy-start | bytes 30724
  0.0 6.0 %copy-start.7 = (f32[1280]{0:T(1024)S(1)}, f32[1280]{0:T(1024)}, u32[]{:S(2)}) copy-start(f32[1280]{0:T(1024)} %param.23) | copy-start | bytes 15364
  0.0 5.4 %copy-start.6 = (f32[1280]{0:T(1024)S(1)}, f32[1280]{0:T(1024)}, u32[]{:S(2)}) copy-start(f32[1280]{0:T(1024)} %param.22) | copy-start | bytes 15364
  0.0 4.8 %copy-start.5 = (f32[1280]{0:T(1024)S(1)}, f32[1280]{0:T(1024)}, u32[]{:S(2)}) copy-start(f32[1280]{0:T(1024)} %param.21) | copy-start | bytes 15364
  0.0 8.1 %copy-start.3 = (f32[1280]{0:T(1024)S(1)}, f32[1280]{0:T(1024)}, u32[]{:S(2)}) copy-start(f32[1280]{0:T(1024)} %param.17) | copy-start | bytes 15364
  0.1 8.1 %copy-start.4 = (f32[1280]{0:T(1024)S(1)}, f32[1280]{0:T(1024)}, u32[]{:S(2)}) copy-start(f32[1280]{0:T(1024)} %param.16) | copy-start | bytes 15364
  9.4 111.5 %copy-start.8 = (f32[1280]{0:T(1024)S(1)}, f32[1280]{0:T(1024)}, u32[]{:S(2)}) copy-start(f32[1280]{0:T(1024)} %param.27) | copy-start | bytes 15364
where the time goes:
time: 128 us; the launch traced here: 127 us
  Pallas kernels  111 us (87%)
  matrix products  6.6 us (5%)
  local copies, waits for them, and re-layouts  5.32 us (4%)
  other arithmetic  3.98 us (3%)
    pallas_call x1, Pallas kernels, layer_until_hidden(): pl.pallas_call(functools.partial(layer_kernel, n, n_dp, heads, HEAD_DIM,...  111 us
    dot_general x1, matrix products, fold_rows(): return jnp.dot(left_side, shard_piece, preferred_element_type=jnp.float32)  6.6 us

commit v1 on v0

v1 whole, which is shorter than its diff:
```python
import functools
import math

import jax
import jax.numpy as jnp
from jax import lax
from jax.experimental import pallas as pl
from jax.experimental.pallas import tpu as pltpu
from jax.sharding import PartitionSpec as P

HEADS = 16
HEAD_DIM = 80
LANES = 128
EPSILON = 1e-05
MESH = pl.DeviceIdType.MESH
HALF = jnp.bfloat16
NORM_ROWS = 48


def up_to(value, step):
    return -(-value // step) * step


class Plan:
    def __init__(self, n, n_dp, images, tok, width, hidden, qkv_width):
        self.n, self.n_dp, self.images, self.tok = n, n_dp, images, tok
        self.width, self.hidden, self.qkv_width = width, hidden, qkv_width
        self.pairs = n_dp // 2
        self.groups = 2 * images
        self.across = n // self.groups
        self.heads = HEADS // (2 * self.across)
        self.length = n * tok
        self.part_heads = self.heads // 2
        self.span = self.part_heads * HEAD_DIM
        self.part_columns = self.part_heads * 3 * LANES
        columns = self.heads * 3 * HEAD_DIM
        starts = [g * columns for g in range(2 * self.across)]
        rest = max(start % LANES for start in starts)
        self.window = up_to(rest + columns, LANES)
        last = starts[-1] // LANES * LANES
        self.shift_back = max(0, last + self.window - qkv_width)
        firsts = [start // LANES * LANES for start in starts]
        firsts[-1] -= self.shift_back
        self.rests = [start - first for start, first in zip(starts, firsts)]
        self.columns = columns
        cut = min(self.window, up_to(max(self.rests) + columns // 2, LANES))
        self.cuts = (0, cut, self.window) if cut < self.window else (0, cut)
        self.q_rows = width // n_dp


def normalize(features, gain, shift):
    average = jnp.mean(features, axis=-1, keepdims=True)
    centered = features - average
    spread = jnp.mean(centered * centered, axis=-1, keepdims=True)
    return centered * lax.rsqrt(spread + EPSILON) * gain + shift


def pieces_of(plan):
    half_out, half_up = plan.width // 2, plan.hidden // 2
    cut = up_to(half_out // 2, LANES)
    return (
        (0, 0, half_out, 0),
        (1, 0, half_up // 2, 0),
        (1, half_up // 2, half_up // 2, 0),
        (2, 0, cut, 1),
        (2, cut, half_out - cut, 1),
    )


def layer_kernel(
    plan,
    tok_ref,
    wq_ref,
    wo_ref,
    wu_ref,
    wd_ref,
    pg_ref,
    ps_ref,
    qb_ref,
    ob_ref,
    mg_ref,
    ms_ref,
    ub_ref,
    db_ref,
    o_ref,
    xin,
    xn,
    wraw,
    wbuf,
    bpad,
    packed,
    mixed,
    landed,
    ctx,
    mid,
    hid,
    w_out,
    w_up,
    w_down,
    t_send,
    t_recv,
    ty_send,
    ty_recv,
    ts_send,
    ts_recv,
    q_send,
    q_recv,
    qz_send,
    qz_recv,
    qs_send,
    qs_recv,
    q_own,
    x_send,
    x_recv,
    p_send,
    p_recv,
    s_send,
    s_recv,
    so_send,
    so_recv,
    own_sem,
    c_send,
    c_recv,
):
    n, n_dp, images, tok = plan.n, plan.n_dp, plan.images, plan.tok
    groups, across, pairs = plan.groups, plan.across, plan.pairs
    d, s = lax.axis_index("dp"), lax.axis_index("seq")
    core = d % 2
    pair = d // 2
    sibling = d + 1 - 2 * core
    z, y = s // across, s % across
    z_near = z + 1 - 2 * (z % 2)
    y_near = y + 1 - 2 * (y % 2)
    z_order = (z, z_near, (z + 2) % groups, (z_near + 2) % groups)
    mine = z // images == core
    others = z // images != core
    shards_of = (wo_ref, wu_ref, wd_ref)
    wholes = (w_out, w_up, w_down)
    pieces = pieces_of(plan)
    n_parts = len(plan.cuts) - 1
    factor = math.log2(math.e) / math.sqrt(HEAD_DIM)

    barrier = pltpu.get_barrier_semaphore()
    for t in range(n):
        if t:
            pl.semaphore_signal(barrier, inc=1, device_id=(d, (s + t) % n), device_id_type=MESH)
        pl.semaphore_signal(barrier, inc=1, device_id=(sibling, (s + t) % n), device_id_type=MESH)
    for j in range(1, pairs):
        for cc in range(2):
            there = (pair + j) % pairs * 2 + cc
            pl.semaphore_signal(barrier, inc=1, device_id=(there, s), device_id_type=MESH)
    pl.semaphore_wait(barrier, 2 * n - 1 + 2 * (pairs - 1))

    def remote(src, dst, send, recv, device):
        return pltpu.make_async_remote_copy(
            src_ref=src, dst_ref=dst, send_sem=send, recv_sem=recv, device_id=device, device_id_type=MESH
        )

    def token_z(i):
        there = core * images + i
        return remote(tok_ref.at[i], xin.at[s], t_send.at[i], t_recv.at[z], (d, there * across + y))

    def token_z_in(zp):
        slot = xin.at[zp * across + y]
        return remote(slot, slot, t_send.at[0], t_recv.at[zp], (d, s))

    def token_y(zp, dy, src):
        there = z * across + (y + dy) % across
        return remote(src, xin.at[zp * across + y], ty_send.at[zp, dy], ty_recv.at[zp, dy], (d, there))

    def token_y_in(zp, dy):
        slot = xin.at[zp * across + (y + across - dy) % across]
        return remote(slot, slot, ty_send.at[zp, dy], ty_recv.at[zp, dy], (d, s))

    def token_s(sp, src):
        return remote(src, xin.at[sp], ts_send.at[sp], ts_recv.at[sp], (sibling, s))

    def own_tokens():
        return tok_ref.at[z % images]

    def q_first(group):
        return pl.multiple_of(
            group * plan.columns // LANES * LANES - group // (2 * across - 1) * plan.shift_back, LANES
        )

    def q_columns(part, group):
        low, high = plan.cuts[part], plan.cuts[part + 1]
        return pl.ds(pl.multiple_of(q_first(group) + low, LANES), high - low)

    def q_part(part):
        return pl.ds(plan.cuts[part], plan.cuts[part + 1] - plan.cuts[part])

    q_half = plan.q_rows // 2

    def q_slab(owner, half):
        return pl.ds(pl.multiple_of(owner * plan.q_rows + half * q_half, 8), q_half)

    def q_x(part, j, cc):
        half = z % 2
        return remote(
            wq_ref.at[pl.ds(pl.multiple_of(half * q_half, 8), q_half), q_columns(part, 2 * y + cc)],
            wraw.at[q_slab(d, half), q_part(part)],
            q_send.at[part, j, cc],
            q_recv.at[part, j, core],
            ((pair + j) % pairs * 2 + cc, s),
        )

    def q_x_in(part, j, cc):
        slot = wraw.at[q_slab((pair + pairs - j) % pairs * 2 + cc, z % 2), q_part(part)]
        return remote(slot, slot, q_send.at[part, j, cc], q_recv.at[part, j, cc], (d, s))

    def q_z(part, j, cc, arriving=False):
        half = 1 - z % 2 if arriving else z % 2
        slot = wraw.at[q_slab((pair + pairs - j) % pairs * 2 + cc, half), q_part(part)]
        there = z_near * across + y
        return remote(slot, slot, qz_send.at[part, j, cc], qz_recv.at[part, j, cc], (d, there))

    def q_full(owner):
        return pl.ds(pl.multiple_of(owner * plan.q_rows, 16), plan.q_rows)

    def q_s(part, arriving=False):
        return remote(
            wq_ref.at[:, q_columns(part, 2 * y + 1 - core)],
            wraw.at[q_full(sibling if arriving else d), q_part(part)],
            qs_send.at[part],
            qs_recv.at[part],
            (sibling, s),
        )

    def q_mine(part):
        return pltpu.make_async_copy(
            wq_ref.at[:, q_columns(part, 2 * y + core)], wraw.at[q_full(d), q_part(part)], q_own.at[part]
        )

    def slab(k, owner):
        depth = shards_of[k].shape[0]
        return pl.ds(pl.multiple_of(owner * depth, 16), depth)

    def piece_columns(piece, other=False):
        k, low, columns, along_z = piece
        half = z % 2 if along_z else y % 2
        if other:
            half = 1 - half
        return pl.ds(pl.multiple_of(half * (wholes[k].shape[1] // 2) + low, LANES), columns)

    def owner_of(j):
        return (pair + pairs - j) % pairs * 2 + core

    def w_x(q, j, arriving=False):
        k = pieces[q][0]
        columns = piece_columns(pieces[q])
        return remote(
            shards_of[k].at[:, columns],
            wholes[k].at[slab(k, owner_of(j) if arriving else d), columns],
            x_send.at[q, j],
            x_recv.at[q, j],
            ((pair + j) % pairs * 2 + core, s),
        )

    def w_p(q, j, arriving=False):
        k, along_z = pieces[q][0], pieces[q][3]
        slot = wholes[k].at[slab(k, owner_of(j)), piece_columns(pieces[q], arriving)]
        there = z_near * across + y if along_z else z * across + y_near
        return remote(slot, slot, p_send.at[q, j], p_recv.at[q, j], (d, there))

    def w_s(q, j, second, arriving=False):
        k = pieces[q][0]
        owner = (pair + pairs - j) % pairs * 2 + (1 - core if arriving else core)
        slot = wholes[k].at[slab(k, owner), piece_columns(pieces[q], second)]
        way = 1 if second else 0
        return remote(slot, slot, s_send.at[q, j, way], s_recv.at[q, j, way], (sibling, s))

    def w_so(k, arriving=False):
        return remote(
            shards_of[k],
            wholes[k].at[slab(k, sibling if arriving else d)],
            so_send.at[k],
            so_recv.at[k],
            (sibling, s),
        )

    def w_own(k):
        return pltpu.make_async_copy(shards_of[k], wholes[k].at[slab(k, d)], own_sem.at[k])

    def pass_first(q):
        for j in range(1, pairs):
            w_x(q, j, True).wait_recv()
            w_p(q, j).start()
            w_s(q, j, False).start()

    def pass_second(q):
        for j in range(1, pairs):
            w_p(q, j, True).wait_recv()
            w_s(q, j, True).start()

    def arrived(k):
        w_own(k).wait()
        w_so(k, True).wait_recv()
        for q, piece in enumerate(pieces):
            if piece[0] == k:
                for j in range(1, pairs):
                    for second in (False, True):
                        w_s(q, j, second, True).wait_recv()

    def ctx_copy(part, sp, group, slot):
        return remote(
            mixed.at[part, sp],
            landed.at[part, group, slot],
            c_send.at[part, sp],
            c_recv.at[part, group, slot],
            (pair * 2 + z // images, sp),
        )

    for k in range(images):
        i = (1 - core) * k + core * (images - 1 - k)

        @pl.when(core * images + i != z)
        def _():
            token_z(i).start()

    @pl.when(mine)
    def _():
        for dy in range(1, across):
            token_y(z, dy, own_tokens()).start()
        token_s(s, own_tokens()).start()

    for part in range(n_parts):
        for j in range(1, pairs):
            q_x(part, j, 0).start()
            q_x(part, j, 1).start()
    for part in range(n_parts):
        q_mine(part).start()
        q_s(part).start()
    for q in range(len(pieces)):
        for j in range(1, pairs):
            w_x(q, j).start()

    wbuf[...] = jnp.zeros_like(wbuf)
    group = 2 * y + core
    per_part = plan.part_heads * 3
    for rest in sorted(set(plan.rests)):
        which = [g for g, r in enumerate(plan.rests) if r == rest]
        hit = group == which[0]
        for g in which[1:]:
            hit = jnp.logical_or(hit, group == g)

        @pl.when(hit)
        def _(rest=rest):
            row = qb_ref[:, pl.ds(q_first(group), plan.window)]
            for g in range(2 * per_part):
                piece = row[:, rest + g * HEAD_DIM : rest + (g + 1) * HEAD_DIM]
                at = g % per_part * LANES
                ones = jnp.full((1, LANES - HEAD_DIM), 1.0 if g % 3 == 2 else 0.0, jnp.float32)
                bpad[g // per_part, :, at : at + LANES] = jnp.concatenate([piece, ones], axis=-1)

    def norm_block(zp):
        rows = across * tok

        def chunk(i, carry):
            at = pl.ds(pl.multiple_of(zp * rows + i * NORM_ROWS, 16), NORM_ROWS)
            per = tok // NORM_ROWS
            inside = pl.ds(pl.multiple_of(i % per * NORM_ROWS, 16), NORM_ROWS)
            block = xin[zp * across + i // per, inside, :].astype(jnp.float32)
            xn[at, :] = normalize(block, pg_ref[...], ps_ref[...]).astype(HALF)
            return carry

        lax.fori_loop(0, rows // NORM_ROWS, chunk, 0)

    @pl.when(mine)
    def _():
        xin[s] = tok_ref[z % images]
        for dy in range(1, across):
            token_y_in(z, dy).wait_recv()
            slot = z * across + (y + across - dy) % across
            token_s(slot, xin.at[slot]).start()

    @pl.when(others)
    def _():
        for yy in range(across):
            slot = z * across + yy
            token_s(slot, xin.at[slot]).wait_recv()

    norm_block(z)
    for step in range(1, groups):
        zp = z_order[step]
        slot = zp * across + y

        @pl.when(mine)
        def _():
            token_z_in(zp).wait_recv()
            for dy in range(1, across):
                token_y(zp, dy, xin.at[slot]).start()
            token_s(slot, xin.at[slot]).start()

        if step - 1 < n_parts:
            for j in range(1, pairs):
                for cc in range(2):
                    q_x_in(step - 1, j, cc).wait_recv()
                    q_z(step - 1, j, cc).start()

        def finish(zq):
            @pl.when(mine)
            def _():
                for dy in range(1, across):
                    token_y_in(zq, dy).wait_recv()
                    other = zq * across + (y + across - dy) % across
                    token_s(other, xin.at[other]).start()

            @pl.when(others)
            def _():
                for yy in range(across):
                    one = zq * across + yy
                    token_s(one, xin.at[one]).wait_recv()

            norm_block(zq)

        if step > 1:
            finish(z_order[step - 1])
        if step == groups - 1:
            finish(zp)

    for k in range(3):
        w_own(k).start()
        w_so(k).start()

    def build(part):
        q_mine(part).wait()
        q_s(part, True).wait_recv()
        for j in range(1, pairs):
            for cc in range(2):
                q_z(part, j, cc, True).wait_recv()

    def pad_weights(part):
        for rest in sorted(set(plan.rests)):
            which = [g for g, r in enumerate(plan.rests) if r == rest]
            hit = group == which[0]
            for g in which[1:]:
                hit = jnp.logical_or(hit, group == g)

            @pl.when(hit)
            def _(rest=rest):
                for g in range(per_part):
                    low = rest + (part * per_part + g) * HEAD_DIM
                    wbuf[part, :, g * LANES : g * LANES + HEAD_DIM] = wraw[:, low : low + HEAD_DIM]

    block_rows = across * tok

    def project(part):
        def one(i, carry):
            at = pl.ds(pl.multiple_of(i * block_rows, 16), block_rows)
            result = jnp.dot(xn[at, :], wbuf[part], preferred_element_type=jnp.float32) + bpad[part]
            packed[part, at, :] = result.astype(HALF)
            return carry

        lax.fori_loop(0, groups, one, 0)

    def attend(part, after):
        def one(step, carry):
            near = (step + 1) // 2 % 2
            far = 1 - step // 2
            zp = (z + near * (1 - 2 * (z % 2)) + 2 * far) % groups
            at = pl.ds(pl.multiple_of(zp * block_rows, 16), block_rows)
            outs = []
            for h in range(plan.part_heads):
                base = h * 3 * LANES
                queries = packed[part, at, base : base + LANES]
                key_rows = packed[part, :, base + LANES : base + 2 * LANES]
                value_rows = packed[part, :, base + 2 * LANES : base + 3 * LANES]
                scores = lax.dot_general(
                    queries, key_rows, (((1,), (1,)), ((), ())), preferred_element_type=jnp.float32
                )
                highest = jnp.max(scores, axis=-1, keepdims=True)
                weights = jnp.exp2((scores - highest) * factor).astype(HALF)
                summed = jnp.dot(weights, value_rows, preferred_element_type=jnp.float32)
                outs.append(summed[:, :HEAD_DIM] / summed[:, HEAD_DIM : HEAD_DIM + 1])
            whole = (jnp.concatenate(outs, axis=-1) if len(outs) > 1 else outs[0]).astype(HALF)
            for yy in range(across):
                sp = zp * across + yy
                mixed[part, sp] = whole[yy * tok : (yy + 1) * tok]
                own = jnp.logical_and(mine, sp == s)

                @pl.when(own)
                def _():
                    landed[part, group, z % images] = whole[yy * tok : (yy + 1) * tok]

                @pl.when(jnp.logical_not(own))
                def _():
                    ctx_copy(part, sp, group, z % images).start()

            for when, action in after:

                @pl.when(step == when)
                def _():
                    action()

            return carry

        lax.fori_loop(0, groups, one, 0)

    build(0)
    pad_weights(0)
    project(0)
    pass_first(0)
    attend(0, [(1, lambda: pass_second(0))])
    build(1)
    pad_weights(1)
    project(1)
    pass_first(1)
    attend(1, [(2, lambda: pass_second(1))])

    pass_first(2)

    def context_in(part, gg, i):
        yy, cc = gg // 2, gg % 2
        source = (core * images + i) * across + yy
        own = jnp.logical_and(source == s, core == cc)
        slot = landed.at[part, gg, i]

        @pl.when(jnp.logical_not(own))
        def _():
            remote(
                mixed.at[part, 0], slot, c_send.at[part, 0], c_recv.at[part, gg, i], (pair * 2 + cc, source)
            ).wait_recv()

    for part in range(2):
        for i in range(images):
            for gg in range(2 * across):
                context_in(part, gg, i)
                low = gg * plan.heads * HEAD_DIM + part * plan.span
                ctx[i * tok : (i + 1) * tok, low : low + plan.span] = landed[part, gg, i]

    pass_second(2)
    arrived(0)
    row_count = images * tok

    def tile_of(c):
        return pl.ds(pl.multiple_of(c * 2 * LANES, 2 * LANES), 2 * LANES)

    def out_tile(c, carry):
        cols = tile_of(c)
        attended = jnp.dot(ctx[...], w_out[:, cols], preferred_element_type=jnp.float32)
        residual = tok_ref[:, :, cols].astype(jnp.float32).reshape(row_count, 2 * LANES)
        mid[:, cols] = residual + attended + ob_ref[:, cols]
        return carry

    lax.fori_loop(0, plan.width // (2 * LANES), out_tile, 0)

    def second_norm(i, carry):
        at = pl.ds(pl.multiple_of(i * NORM_ROWS, 16), NORM_ROWS)
        ctx[at, :] = normalize(mid[at, :], mg_ref[...], ms_ref[...]).astype(HALF)
        return carry

    lax.fori_loop(0, row_count // NORM_ROWS, second_norm, 0)
    arrived(1)

    def up_tile(c, carry):
        cols = tile_of(c)
        lifted = jnp.dot(ctx[...], w_up[:, cols], preferred_element_type=jnp.float32)
        lifted = lifted + ub_ref[:, cols]
        hid[:, cols] = (0.5 * lifted * (1.0 + lax.erf(lifted * math.sqrt(0.5)))).astype(HALF)
        return carry

    lax.fori_loop(0, plan.hidden // (2 * LANES), up_tile, 0)
    pass_first(3)
    pass_first(4)
    pass_second(3)
    pass_second(4)
    arrived(2)

    def down_tile(c, carry):
        cols = tile_of(c)
        lowered = jnp.dot(hid[...], w_down[:, cols], preferred_element_type=jnp.float32)
        result = (mid[:, cols] + lowered + db_ref[:, cols]).astype(HALF)
        o_ref[:, :, cols] = result.reshape(images, tok, 2 * LANES)
        return carry

    lax.fori_loop(0, plan.width // (2 * LANES), down_tile, 0)

    for k in range(images):

        @pl.when(core * images + k != z)
        def _():
            token_z(k).wait_send()

    @pl.when(mine)
    def _():
        for zp in range(groups):
            slot = zp * across + y
            for dy in range(1, across):
                token_y(zp, dy, xin.at[slot]).wait_send()
        for sp in range(n):
            token_s(sp, xin.at[sp]).wait_send()

    for part in range(n_parts):
        q_s(part).wait_send()
        for j in range(1, pairs):
            for cc in range(2):
                q_x(part, j, cc).wait_send()
                q_z(part, j, cc).wait_send()
    for k in range(3):
        w_so(k).wait_send()
    for q in range(len(pieces)):
        for j in range(1, pairs):
            w_x(q, j).wait_send()
            w_p(q, j).wait_send()
            w_s(q, j, False).wait_send()
            w_s(q, j, True).wait_send()
    for part in range(2):
        for sp in range(n):

            @pl.when(jnp.logical_not(jnp.logical_and(mine, sp == s)))
            def _():
                ctx_copy(part, sp, group, z % images).wait_send()


def shards(n, n_dp, tokens, pre_gain, pre_shift, w_qkv, qkv_bias, w_out, out_bias, mlp_gain, mlp_shift,
           w_up, up_bias, w_down, down_bias):
    images, tok, width = tokens.shape
    hidden = w_up.shape[1]
    plan = Plan(n, n_dp, images, tok, width, hidden, w_qkv.shape[1])
    rows = images * tok
    dma = pltpu.SemaphoreType.DMA
    vmem = pl.BlockSpec(memory_space=pltpu.VMEM)
    anywhere = pl.BlockSpec(memory_space=pl.ANY)
    pairs, groups, across = plan.pairs, plan.groups, plan.across
    n_pieces = len(pieces_of(plan))
    parts = len(plan.cuts) - 1
    return pl.pallas_call(
        functools.partial(layer_kernel, plan),
        out_shape=jax.ShapeDtypeStruct(tokens.shape, HALF),
        in_specs=[vmem] + [anywhere] * 4 + [vmem] * 8,
        out_specs=vmem,
        scratch_shapes=[
            pltpu.VMEM((n, tok, width), HALF),
            pltpu.VMEM((plan.length, width), HALF),
            pltpu.VMEM((width, plan.window), HALF),
            pltpu.VMEM((2, width, plan.part_columns), HALF),
            pltpu.VMEM((2, 1, plan.part_columns), jnp.float32),
            pltpu.VMEM((2, plan.length, plan.part_columns), HALF),
            pltpu.VMEM((2, n, tok, plan.span), HALF),
            pltpu.VMEM((2, 2 * across, images, tok, plan.span), HALF),
            pltpu.VMEM((rows, width), HALF),
            pltpu.VMEM((rows, width), jnp.float32),
            pltpu.VMEM((rows, hidden), HALF),
            pltpu.VMEM((width, width), HALF),
            pltpu.VMEM((width, hidden), HALF),
            pltpu.VMEM((hidden, width), HALF),
            dma((images,)),
            dma((groups,)),
            dma((groups, across)),
            dma((groups, across)),
            dma((n,)),
            dma((n,)),
            dma((parts, pairs, 2)),
            dma((parts, pairs, 2)),
            dma((parts, pairs, 2)),
            dma((parts, pairs, 2)),
            dma((parts,)),
            dma((parts,)),
            dma((parts,)),
            dma((n_pieces, pairs)),
            dma((n_pieces, pairs)),
            dma((n_pieces, pairs)),
            dma((n_pieces, pairs)),
            dma((n_pieces, pairs, 2)),
            dma((n_pieces, pairs, 2)),
            dma((3,)),
            dma((3,)),
            dma((3,)),
            dma((2, n)),
            dma((2, 2 * across, images)),
        ],
        compiler_params=pltpu.CompilerParams(
            collective_id=0, has_side_effects=True, vmem_limit_bytes=60 * 1024 * 1024
        ),
        name="encoder_layer",
    )(
        tokens,
        w_qkv,
        w_out,
        w_up,
        w_down,
        pre_gain[None],
        pre_shift[None],
        qkv_bias[None],
        out_bias[None],
        mlp_gain[None],
        mlp_shift[None],
        up_bias[None],
        down_bias[None],
    )


def solution(mesh):
    in_specs = (
        P("dp", "seq", None),
        P(),
        P(),
        P("dp", None),
        P(),
        P("dp", None),
        P(),
        P(),
        P(),
        P("dp", None),
        P(),
        P("dp", None),
        P(),
    )
    out_specs = P("dp", "seq", None)
    step = functools.partial(shards, mesh.shape["seq"], mesh.shape["dp"])
    return jax.shard_map(step, mesh=mesh, in_specs=in_specs, out_specs=out_specs, check_vma=False)
```

time: 128 us -> 134 us (1.047)
  Pallas kernels: 111 us -> 120 us
  local copies, waits for them, and re-layouts: 5.32 us -> 12.4 us
  matrix products: 6.6 us -> 0 us
  other arithmetic: 3.98 us -> 0 us
    pallas_call x1, Pallas kernels: 111 us -> 120 us  [shards(): pl.pallas_call(functools.partial(layer_kernel, plan), out_shape=jax.Shape...]
    dot_general x1 -> x0, matrix products: 6.6 us -> none  [fold_rows(): return jnp.dot(left_side, shard_piece, preferred_element_type=jnp.float32)]
    broadcast_in_dim x0 -> x4, local copies, waits for them, and re-layouts: none -> 5.17 us  [the longest x1 1.33 us: shards(): qkv_bias[None]]
    reduce_sum x2 -> x0, other arithmetic: 2.75 us -> none  [the longest x1 1.45 us: normalize(): spread = jnp.mean(centered * centered, axis=-1, keepdims=True)]
    unnamed x18 -> x1, local copies, waits for them, and re-layouts: 0.04 us -> 2.03 us
where the time goes in v1:
time: 134 us; the launch traced here: 132 us
  Pallas kernels  120 us (90%)
  local copies, waits for them, and re-layouts  12.4 us (9%)
    pallas_call x1, Pallas kernels, shards(): pl.pallas_call(functools.partial(layer_kernel, plan), out_shape=jax.Shape...  120 us

profile of v1, /device:TPU:1, one launch (start us, length us, event | category | flops | bytes accessed | tf_op | source)
XLA Modules:
  0.0 132.5 jit_solution(3270691889233632600)
XLA Ops:
  0.0 1.3 broadcast_in_dim.24.pg_ref
  1.3 1.3 broadcast_in_dim.25.ps_ref
  2.6 1.3 broadcast_in_dim.27.ob_ref
  3.9 1.3 broadcast_in_dim.28.mg_ref
  5.1 1.3 broadcast_in_dim.29.ms_ref
  6.4 1.3 broadcast_in_dim.31.db_ref
  7.7 1.3 broadcast_in_dim.30.ub_ref
  9.0 1.3 %broadcast_in_dim.26.qb_ref = f32[1,3840]{1,0:T(1,128)} reshape(f32[3840]{0:T(1024)} %param.17) | data formatting | bytes 30720 | tf_op jit(solution)/shard_map/broadcast_in_dim | solution.py:685
  10.4 120.1 %encoder_layer.1 = bf16[2,144,1280]{2,1,0:T(8,128)(2,1)} custom-call(bf16[2,144,1280]{2,1,0:T(8,128)(2,1)} %tok_ref.1, bf16[320,3840]{1,0:T(8,128)(2,1)} %wq_ref.1, bf16[320,1280]{1,0:T(8,128)(2,1)} %wo_ref.1, bf16[320,2560]{1,0:T(8,128)(2,1)} %wu_ref.1, bf16[640,1280]{1,0:T(8,128)(2,1)} %wd_ref.1, f32[1,1280]{1,0:T(1,128)} %broadcast_in_dim.24.pg_ref, ...), custom_call_target="tpu_custom_call" | custom-call | tf_op jit(solution)/shard_map/encoder_layer/pallas_call | solution.py:628
  130.4 2.0 %copy.15 = bf16[2,144,1280]{2,1,0:T(8,128)(2,1)} copy(bf16[2,144,1280]{2,1,0:T(8,128)(2,1)} %encoder_layer.1) | data formatting | bytes 1474560

commit v2 on v1

--- a/solution.py
+++ b/solution.py
@@ -32,6 +32,8 @@
         self.length = n * tok
         self.part_heads = self.heads // 2
         self.span = self.part_heads * HEAD_DIM
+        early = self.span // LANES * LANES
+        self.sends = ((0, early), (early, 2 * self.span))
         self.part_columns = self.part_heads * 3 * LANES
         columns = self.heads * 3 * HEAD_DIM
         starts = [g * columns for g in range(2 * self.across)]
@@ -55,25 +57,37 @@
     return centered * lax.rsqrt(spread + EPSILON) * gain + shift
 
 
+def thirds(columns, parts):
+    tiles = columns // LANES
+    sizes = [(tiles + parts - 1 - p) // parts * LANES for p in range(parts)]
+    return [(sum(sizes[:p]), size) for p, size in enumerate(sizes) if size]
+
+
 def pieces_of(plan):
-    half_out, half_up = plan.width // 2, plan.hidden // 2
-    cut = up_to(half_out // 2, LANES)
-    return (
-        (0, 0, half_out, 0),
-        (1, 0, half_up // 2, 0),
-        (1, half_up // 2, half_up // 2, 0),
-        (2, 0, cut, 1),
-        (2, cut, half_out - cut, 1),
-    )
+    cuts = (thirds(plan.width // 2, 1), thirds(plan.hidden // 2, 4), thirds(plan.width // 2, 3))
+    along = ((0,), (0, 0, 0, 1), (1, 0, 1))
+    return tuple((k, low, size, along[k][p]) for k in range(3) for p, (low, size) in enumerate(cuts[k]))
 
 
 def layer_kernel(
     plan,
-    tok_ref,
+    tok_in,
     wq_ref,
     wo_ref,
     wu_ref,
     wd_ref,
+    pg_in,
+    ps_in,
+    qb_in,
+    ob_in,
+    mg_in,
+    ms_in,
+    ub_in,
+    db_in,
+    o_out,
+    tok_ref,
+    o_ref,
+    io_sem,
     pg_ref,
     ps_ref,
     qb_ref,
@@ -82,7 +96,7 @@
     ms_ref,
     ub_ref,
     db_ref,
-    o_ref,
+    vec_sem,
     xin,
     xn,
     wraw,
@@ -140,6 +154,14 @@
     n_parts = len(plan.cuts) - 1
     factor = math.log2(math.e) / math.sqrt(HEAD_DIM)
 
+    vectors = ((pg_in, pg_ref), (ps_in, ps_ref), (qb_in, qb_ref), (ob_in, ob_ref))
+    vectors += ((mg_in, mg_ref), (ms_in, ms_ref), (ub_in, ub_ref), (db_in, db_ref))
+    vector_copies = [pltpu.make_async_copy(a, b.at[0], vec_sem.at[v]) for v, (a, b) in enumerate(vectors)]
+    token_copy = pltpu.make_async_copy(tok_in, tok_ref, io_sem.at[0])
+    token_copy.start()
+    for copy in vector_copies:
+        copy.start()
+
     barrier = pltpu.get_barrier_semaphore()
     for t in range(n):
         if t:
@@ -156,27 +178,45 @@
             src_ref=src, dst_ref=dst, send_sem=send, recv_sem=recv, device_id=device, device_id_type=MESH
         )
 
-    def token_z(i):
+    chunks = tok // NORM_ROWS
+
+    def rows_at(c):
+        return pl.ds(c * NORM_ROWS, NORM_ROWS)
+
+    def token_z(i, c):
         there = core * images + i
-        return remote(tok_ref.at[i], xin.at[s], t_send.at[i], t_recv.at[z], (d, there * across + y))
-
-    def token_z_in(zp):
-        slot = xin.at[zp * across + y]
-        return remote(slot, slot, t_send.at[0], t_recv.at[zp], (d, s))
-
-    def token_y(zp, dy, src):
+        return remote(
+            tok_ref.at[i, rows_at(c)],
+            xin.at[s, rows_at(c)],
+            t_send.at[i, c],
+            t_recv.at[z, c],
+            (d, there * across + y),
+        )
+
+    def token_z_in(zp, c):
+        slot = xin.at[zp * across + y, rows_at(c)]
+        return remote(slot, slot, t_send.at[0, c], t_recv.at[zp, c], (d, s))
+
+    def token_y(zp, dy, c, src=None):
         there = z * across + (y + dy) % across
-        return remote(src, xin.at[zp * across + y], ty_send.at[zp, dy], ty_recv.at[zp, dy], (d, there))
-
-    def token_y_in(zp, dy):
-        slot = xin.at[zp * across + (y + across - dy) % across]
-        return remote(slot, slot, ty_send.at[zp, dy], ty_recv.at[zp, dy], (d, s))
-
-    def token_s(sp, src):
-        return remote(src, xin.at[sp], ts_send.at[sp], ts_recv.at[sp], (sibling, s))
-
-    def own_tokens():
-        return tok_ref.at[z % images]
+        slot = xin.at[zp * across + y, rows_at(c)]
+        return remote(
+            slot if src is None else src, slot, ty_send.at[zp, dy, c], ty_recv.at[zp, dy, c], (d, there)
+        )
+
+    def side_slot(zp, dy):
+        return zp * across + (y + across - dy) % across
+
+    def token_y_in(zp, dy, c):
+        slot = xin.at[side_slot(zp, dy), rows_at(c)]
+        return remote(slot, slot, ty_send.at[zp, dy, c], ty_recv.at[zp, dy, c], (d, s))
+
+    def token_s(sp, c, src=None):
+        slot = xin.at[sp, rows_at(c)]
+        return remote(slot if src is None else src, slot, ts_send.at[sp, c], ts_recv.at[sp, c], (sibling, s))
+
+    def own_tokens(c):
+        return tok_ref.at[z % images, rows_at(c)]
 
     def q_first(group):
         return pl.multiple_of(
@@ -303,39 +343,55 @@
                         w_s(q, j, second, True).wait_recv()
 
     def ctx_copy(part, sp, group, slot):
+        low, high = plan.sends[part]
         return remote(
-            mixed.at[part, sp],
-            landed.at[part, group, slot],
+            mixed.at[sp, :, pl.ds(low, high - low)],
+            landed.at[group, slot, :, pl.ds(low, high - low)],
             c_send.at[part, sp],
             c_recv.at[part, group, slot],
             (pair * 2 + z // images, sp),
         )
 
-    for k in range(images):
-        i = (1 - core) * k + core * (images - 1 - k)
-
-        @pl.when(core * images + i != z)
+    def sends_in(part):
+        return plan.sends[part][0] < plan.sends[part][1]
+
+    token_copy.wait()
+    for c in range(chunks):
+        for k in range(images):
+            i = (1 - core) * k + core * (images - 1 - k)
+
+            @pl.when(core * images + i != z)
+            def _():
+                token_z(i, c).start()
+
+        @pl.when(mine)
         def _():
-            token_z(i).start()
-
-    @pl.when(mine)
-    def _():
-        for dy in range(1, across):
-            token_y(z, dy, own_tokens()).start()
-        token_s(s, own_tokens()).start()
-
-    for part in range(n_parts):
+            for dy in range(1, across):
+                token_y(z, dy, c, own_tokens(c)).start()
+            token_s(s, c, own_tokens(c)).start()
+
+    def q_start(part):
         for j in range(1, pairs):
             q_x(part, j, 0).start()
             q_x(part, j, 1).start()
+
+    def w_start(q):
+        for j in range(1, pairs):
+            w_x(q, j).start()
+
+    q_start(0)
+    w_start(0)
+    for part in range(1, n_parts):
+        q_start(part)
     for part in range(n_parts):
         q_mine(part).start()
         q_s(part).start()
-    for q in range(len(pieces)):
-        for j in range(1, pairs):
-            w_x(q, j).start()
+    for q in range(1, len(pieces)):
+        w_start(q)
 
     wbuf[...] = jnp.zeros_like(wbuf)
+    for copy in vector_copies:
+        copy.wait()
     group = 2 * y + core
     per_part = plan.part_heads * 3
     for rest in sorted(set(plan.rests)):
@@ -353,84 +409,10 @@
                 ones = jnp.full((1, LANES - HEAD_DIM), 1.0 if g % 3 == 2 else 0.0, jnp.float32)
                 bpad[g // per_part, :, at : at + LANES] = jnp.concatenate([piece, ones], axis=-1)
 
-    def norm_block(zp):
-        rows = across * tok
-
-        def chunk(i, carry):
-            at = pl.ds(pl.multiple_of(zp * rows + i * NORM_ROWS, 16), NORM_ROWS)
-            per = tok // NORM_ROWS
-            inside = pl.ds(pl.multiple_of(i % per * NORM_ROWS, 16), NORM_ROWS)
-            block = xin[zp * across + i // per, inside, :].astype(jnp.float32)
-            xn[at, :] = normalize(block, pg_ref[...], ps_ref[...]).astype(HALF)
-            return carry
-
-        lax.fori_loop(0, rows // NORM_ROWS, chunk, 0)
-
-    @pl.when(mine)
-    def _():
-        xin[s] = tok_ref[z % images]
-        for dy in range(1, across):
-            token_y_in(z, dy).wait_recv()
-            slot = z * across + (y + across - dy) % across
-            token_s(slot, xin.at[slot]).start()
-
-    @pl.when(others)
-    def _():
-        for yy in range(across):
-            slot = z * across + yy
-            token_s(slot, xin.at[slot]).wait_recv()
-
-    norm_block(z)
-    for step in range(1, groups):
-        zp = z_order[step]
-        slot = zp * across + y
-
-        @pl.when(mine)
-        def _():
-            token_z_in(zp).wait_recv()
-            for dy in range(1, across):
-                token_y(zp, dy, xin.at[slot]).start()
-            token_s(slot, xin.at[slot]).start()
-
-        if step - 1 < n_parts:
-            for j in range(1, pairs):
-                for cc in range(2):
-                    q_x_in(step - 1, j, cc).wait_recv()
-                    q_z(step - 1, j, cc).start()
-
-        def finish(zq):
-            @pl.when(mine)
-            def _():
-                for dy in range(1, across):
-                    token_y_in(zq, dy).wait_recv()
-                    other = zq * across + (y + across - dy) % across
-                    token_s(other, xin.at[other]).start()
-
-            @pl.when(others)
-            def _():
-                for yy in range(across):
-                    one = zq * across + yy
-                    token_s(one, xin.at[one]).wait_recv()
-
-            norm_block(zq)
-
-        if step > 1:
-            finish(z_order[step - 1])
-        if step == groups - 1:
-            finish(zp)
-
-    for k in range(3):
-        w_own(k).start()
-        w_so(k).start()
-
-    def build(part):
-        q_mine(part).wait()
-        q_s(part, True).wait_recv()
-        for j in range(1, pairs):
-            for cc in range(2):
-                q_z(part, j, cc, True).wait_recv()
-
-    def pad_weights(part):
+    pair_rows = 2 * plan.q_rows
+
+    def pad_weights(part, j):
+        rows = pl.ds(pl.multiple_of((pair + j) % pairs * pair_rows, 16), pair_rows)
         for rest in sorted(set(plan.rests)):
             which = [g for g, r in enumerate(plan.rests) if r == rest]
             hit = group == which[0]
@@ -441,7 +423,98 @@
             def _(rest=rest):
                 for g in range(per_part):
                     low = rest + (part * per_part + g) * HEAD_DIM
-                    wbuf[part, :, g * LANES : g * LANES + HEAD_DIM] = wraw[:, low : low + HEAD_DIM]
+                    wbuf[part, rows, g * LANES : g * LANES + HEAD_DIM] = wraw[rows, low : low + HEAD_DIM]
+
+    def pad_others(part):
+        for j in range(1, pairs):
+            for cc in range(2):
+                q_z(part, j, cc, True).wait_recv()
+        for j in range(1, pairs):
+            pad_weights(part, j)
+
+    def pad_own():
+        for part in range(n_parts):
+            q_mine(part).wait()
+            q_s(part, True).wait_recv()
+        for part in range(2):
+            pad_weights(part, 0)
+
+    def norm_chunk(slot, c):
+        at = pl.ds(pl.multiple_of(slot * tok + c * NORM_ROWS, 16), NORM_ROWS)
+        block = xin[slot, rows_at(c), :].astype(jnp.float32)
+        xn[at, :] = normalize(block, pg_ref[...], ps_ref[...]).astype(HALF)
+
+    def side(zp, c):
+        @pl.when(mine)
+        def _():
+            for dy in range(1, across):
+                token_y_in(zp, dy, c).wait_recv()
+                token_s(side_slot(zp, dy), c).start()
+
+        @pl.when(others)
+        def _():
+            for dy in range(1, across):
+                token_s(side_slot(zp, dy), c).wait_recv()
+
+    def norm_side(zp, c):
+        for dy in range(1, across):
+            norm_chunk(side_slot(zp, dy), c)
+
+    def far(zp, c):
+        slot = zp * across + y
+
+        @pl.when(mine)
+        def _():
+            token_z_in(zp, c).wait_recv()
+            for dy in range(1, across):
+                token_y(zp, dy, c).start()
+            token_s(slot, c).start()
+
+        @pl.when(others)
+        def _():
+            token_s(slot, c).wait_recv()
+
+    def q_relay(part):
+        for j in range(1, pairs):
+            for cc in range(2):
+                q_x_in(part, j, cc).wait_recv()
+                q_z(part, j, cc).start()
+
+    @pl.when(mine)
+    def _():
+        xin[s] = tok_ref[z % images]
+
+    @pl.when(others)
+    def _():
+        for c in range(chunks):
+            token_s(s, c).wait_recv()
+
+    for c in range(chunks):
+        norm_chunk(s, c)
+    for c in range(chunks):
+        side(z, c)
+        norm_side(z, c)
+    pad_own()
+    for c in range(chunks):
+        for zp in z_order[1:]:
+            far(zp, c)
+        if c == 0:
+            q_relay(0)
+        if c:
+            for zp in z_order[1:]:
+                side(zp, c - 1)
+        for zp in z_order[1:]:
+            norm_chunk(zp * across + y, c)
+            if c:
+                norm_side(zp, c - 1)
+    pass_first(0)
+    for zp in z_order[1:]:
+        side(zp, chunks - 1)
+        norm_side(zp, chunks - 1)
+
+    for k in range(3):
+        w_own(k).start()
+        w_so(k).start()
 
     block_rows = across * tok
 
@@ -476,16 +549,19 @@
             whole = (jnp.concatenate(outs, axis=-1) if len(outs) > 1 else outs[0]).astype(HALF)
             for yy in range(across):
                 sp = zp * across + yy
-                mixed[part, sp] = whole[yy * tok : (yy + 1) * tok]
+                here = slice(part * plan.span, (part + 1) * plan.span)
+                mixed[sp, :, here] = whole[yy * tok : (yy + 1) * tok]
                 own = jnp.logical_and(mine, sp == s)
 
                 @pl.when(own)
                 def _():
-                    landed[part, group, z % images] = whole[yy * tok : (yy + 1) * tok]
-
-                @pl.when(jnp.logical_not(own))
-                def _():
-                    ctx_copy(part, sp, group, z % images).start()
+                    landed[group, z % images, :, here] = whole[yy * tok : (yy + 1) * tok]
+
+                if sends_in(part):
+
+                    @pl.when(jnp.logical_not(own))
+                    def _():
+                        ctx_copy(part, sp, group, z % images).start()
 
             for when, action in after:
 
@@ -497,39 +573,51 @@
 
         lax.fori_loop(0, groups, one, 0)
 
-    build(0)
-    pad_weights(0)
+    pad_others(0)
     project(0)
-    pass_first(0)
-    attend(0, [(1, lambda: pass_second(0))])
-    build(1)
-    pad_weights(1)
+    for part in range(1, n_parts):
+        q_relay(part)
+    attend(0, [])
+    pass_first(1)
+    pad_others(1)
     project(1)
-    pass_first(1)
-    attend(1, [(2, lambda: pass_second(1))])
-
+    attend(1, [])
     pass_first(2)
+    pass_first(3)
+    pass_first(4)
 
     def context_in(part, gg, i):
+        if not sends_in(part):
+            return
         yy, cc = gg // 2, gg % 2
         source = (core * images + i) * across + yy
         own = jnp.logical_and(source == s, core == cc)
-        slot = landed.at[part, gg, i]
+        low, high = plan.sends[part]
+        slot = landed.at[gg, i, :, pl.ds(low, high - low)]
 
         @pl.when(jnp.logical_not(own))
         def _():
             remote(
-                mixed.at[part, 0], slot, c_send.at[part, 0], c_recv.at[part, gg, i], (pair * 2 + cc, source)
+                slot, slot, c_send.at[part, 0], c_recv.at[part, gg, i], (pair * 2 + cc, source)
             ).wait_recv()
 
-    for part in range(2):
+    def contexts_in(part):
         for i in range(images):
             for gg in range(2 * across):
                 context_in(part, gg, i)
-                low = gg * plan.heads * HEAD_DIM + part * plan.span
-                ctx[i * tok : (i + 1) * tok, low : low + plan.span] = landed[part, gg, i]
-
-    pass_second(2)
+
+    def gather_contexts():
+        columns = plan.heads * HEAD_DIM
+        for i in range(images):
+            for gg in range(2 * across):
+                ctx[i * tok : (i + 1) * tok, gg * columns : (gg + 1) * columns] = landed[gg, i]
+
+    contexts_in(0)
+    pass_second(0)
+    pass_second(1)
+    pass_first(5)
+    contexts_in(1)
+    gather_contexts()
     arrived(0)
     row_count = images * tok
 
@@ -551,45 +639,69 @@
         return carry
 
     lax.fori_loop(0, row_count // NORM_ROWS, second_norm, 0)
-    arrived(1)
-
-    def up_tile(c, carry):
-        cols = tile_of(c)
+
+    def lift(cols):
         lifted = jnp.dot(ctx[...], w_up[:, cols], preferred_element_type=jnp.float32)
         lifted = lifted + ub_ref[:, cols]
         hid[:, cols] = (0.5 * lifted * (1.0 + lax.erf(lifted * math.sqrt(0.5)))).astype(HALF)
-        return carry
-
-    lax.fori_loop(0, plan.hidden // (2 * LANES), up_tile, 0)
-    pass_first(3)
-    pass_first(4)
-    pass_second(3)
-    pass_second(4)
-    arrived(2)
-
-    def down_tile(c, carry):
-        cols = tile_of(c)
+
+    def piece_in(q, second):
+        for j in range(1, pairs):
+            w_s(q, j, second, True).wait_recv()
+
+    ups = [q for q, piece in enumerate(pieces) if piece[0] == 1]
+    downs = [q for q, piece in enumerate(pieces) if piece[0] == 2]
+    w_own(1).wait()
+    w_so(1, True).wait_recv()
+    for q in ups:
+        piece_in(q, False)
+        lift(piece_columns(pieces[q], False))
+    pass_first(6)
+    for p, q in enumerate(ups[1:]):
+        pass_second(q)
+        before = ups[p]
+        piece_in(before, True)
+        lift(piece_columns(pieces[before], True))
+    pass_first(7)
+    piece_in(ups[-1], True)
+    lift(piece_columns(pieces[ups[-1]], True))
+
+    def result_copy(slot, cols):
+        return pltpu.make_async_copy(o_ref.at[:, :, cols], o_out.at[:, :, cols], io_sem.at[slot + 1])
+
+    def lower(slot, cols):
         lowered = jnp.dot(hid[...], w_down[:, cols], preferred_element_type=jnp.float32)
         result = (mid[:, cols] + lowered + db_ref[:, cols]).astype(HALF)
-        o_ref[:, :, cols] = result.reshape(images, tok, 2 * LANES)
-        return carry
-
-    lax.fori_loop(0, plan.width // (2 * LANES), down_tile, 0)
-
-    for k in range(images):
-
-        @pl.when(core * images + k != z)
+        o_ref[:, :, cols] = result.reshape(images, tok, cols.size)
+        result_copy(slot, cols).start()
+
+    w_own(2).wait()
+    w_so(2, True).wait_recv()
+    for p, q in enumerate(downs):
+        piece_in(q, False)
+        lower(2 * q, piece_columns(pieces[q], False))
+        pass_second(q)
+    for q in downs:
+        piece_in(q, True)
+        lower(2 * q + 1, piece_columns(pieces[q], True))
+    for second in (False, True):
+        for q in downs:
+            result_copy(2 * q + second, piece_columns(pieces[q], second)).wait()
+
+    for c in range(chunks):
+        for k in range(images):
+
+            @pl.when(core * images + k != z)
+            def _():
+                token_z(k, c).wait_send()
+
+        @pl.when(mine)
         def _():
-            token_z(k).wait_send()
-
-    @pl.when(mine)
-    def _():
-        for zp in range(groups):
-            slot = zp * across + y
-            for dy in range(1, across):
-                token_y(zp, dy, xin.at[slot]).wait_send()
-        for sp in range(n):
-            token_s(sp, xin.at[sp]).wait_send()
+            for zp in range(groups):
+                for dy in range(1, across):
+                    token_y(zp, dy, c).wait_send()
+            for sp in range(n):
+                token_s(sp, c).wait_send()
 
     for part in range(n_parts):
         q_s(part).wait_send()
@@ -610,7 +722,8 @@
 
             @pl.when(jnp.logical_not(jnp.logical_and(mine, sp == s)))
             def _():
-                ctx_copy(part, sp, group, z % images).wait_send()
+                if sends_in(part):
+                    ctx_copy(part, sp, group, z % images).wait_send()
 
 
 def shards(n, n_dp, tokens, pre_gain, pre_shift, w_qkv, qkv_bias, w_out, out_bias, mlp_gain, mlp_shift,
@@ -620,37 +733,43 @@
     plan = Plan(n, n_dp, images, tok, width, hidden, w_qkv.shape[1])
     rows = images * tok
     dma = pltpu.SemaphoreType.DMA
-    vmem = pl.BlockSpec(memory_space=pltpu.VMEM)
     anywhere = pl.BlockSpec(memory_space=pl.ANY)
     pairs, groups, across = plan.pairs, plan.groups, plan.across
     n_pieces = len(pieces_of(plan))
     parts = len(plan.cuts) - 1
+    chunks = tok // NORM_ROWS
+    vectors = (pre_gain, pre_shift, qkv_bias, out_bias, mlp_gain, mlp_shift, up_bias, down_bias)
     return pl.pallas_call(
         functools.partial(layer_kernel, plan),
         out_shape=jax.ShapeDtypeStruct(tokens.shape, HALF),
-        in_specs=[vmem] + [anywhere] * 4 + [vmem] * 8,
-        out_specs=vmem,
+        in_specs=[anywhere] * 13,
+        out_specs=anywhere,
         scratch_shapes=[
+            pltpu.VMEM(tokens.shape, HALF),
+            pltpu.VMEM(tokens.shape, HALF),
+            dma((1 + 2 * n_pieces,)),
+            *[pltpu.VMEM((1, v.shape[0]), jnp.float32) for v in vectors],
+            dma((8,)),
             pltpu.VMEM((n, tok, width), HALF),
             pltpu.VMEM((plan.length, width), HALF),
             pltpu.VMEM((width, plan.window), HALF),
             pltpu.VMEM((2, width, plan.part_columns), HALF),
             pltpu.VMEM((2, 1, plan.part_columns), jnp.float32),
             pltpu.VMEM((2, plan.length, plan.part_columns), HALF),
-            pltpu.VMEM((2, n, tok, plan.span), HALF),
-            pltpu.VMEM((2, 2 * across, images, tok, plan.span), HALF),
+            pltpu.VMEM((n, tok, 2 * plan.span), HALF),
+            pltpu.VMEM((2 * across, images, tok, 2 * plan.span), HALF),
             pltpu.VMEM((rows, width), HALF),
             pltpu.VMEM((rows, width), jnp.float32),
             pltpu.VMEM((rows, hidden), HALF),
             pltpu.VMEM((width, width), HALF),
             pltpu.VMEM((width, hidden), HALF),
             pltpu.VMEM((hidden, width), HALF),
-            dma((images,)),
-            dma((groups,)),
-            dma((groups, across)),
-            dma((groups, across)),
-            dma((n,)),
-            dma((n,)),
+            dma((images, chunks)),
+            dma((groups, chunks)),
+            dma((groups, across, chunks)),
+            dma((groups, across, chunks)),
+            dma((n, chunks)),
+            dma((n, chunks)),
             dma((parts, pairs, 2)),
             dma((parts, pairs, 2)),
             dma((parts, pairs, 2)),
@@ -671,7 +790,7 @@
             dma((2, 2 * across, images)),
         ],
         compiler_params=pltpu.CompilerParams(
-            collective_id=0, has_side_effects=True, vmem_limit_bytes=60 * 1024 * 1024
+            collective_id=0, has_side_effects=True, vmem_limit_bytes=67043328
         ),
         name="encoder_layer",
     )(
@@ -680,14 +799,7 @@
         w_out,
         w_up,
         w_down,
-        pre_gain[None],
-        pre_shift[None],
-        qkv_bias[None],
-        out_bias[None],
-        mlp_gain[None],
-        mlp_shift[None],
-        up_bias[None],
-        down_bias[None],
+        *vectors,
     )
 
 

time: 134 us -> 84.3 us (0.63)
  Pallas kernels: 120 us -> 81.7 us
  local copies, waits for them, and re-layouts: 12.4 us -> 2.03 us
    pallas_call x1, Pallas kernels: 120 us -> 81.7 us  [shards(): pl.pallas_call(functools.partial(layer_kernel, plan), out_shape=jax.Shape...]
    broadcast_in_dim x8 -> x0, local copies, waits for them, and re-layouts: 10.4 us -> none  [the longest x1 1.33 us: shards(): qkv_bias[None]]
where the time goes in v2:
time: 84.3 us; the launch traced here: 83.7 us
  Pallas kernels  81.7 us (97%)
  local copies, waits for them, and re-layouts  2.03 us (2%)
    pallas_call x1, Pallas kernels, shards(): pl.pallas_call(functools.partial(layer_kernel, plan), out_shape=jax.Shape...  81.7 us
    unnamed x1, local copies, waits for them, and re-layouts  2.03 us

profile of v2, /device:TPU:1, one launch (start us, length us, event | category | flops | bytes accessed | tf_op | source)
XLA Modules:
  0.0 83.7 jit_solution(13206363471406796820)
XLA Ops:
  0.0 81.7 %encoder_layer.1 = bf16[2,144,1280]{2,1,0:T(8,128)(2,1)} custom-call(bf16[2,144,1280]{2,1,0:T(8,128)(2,1)} %tok_in.1, bf16[320,3840]{1,0:T(8,128)(2,1)} %wq_ref.1, bf16[320,1280]{1,0:T(8,128)(2,1)} %wo_ref.1, bf16[320,2560]{1,0:T(8,128)(2,1)} %wu_ref.1, bf16[640,1280]{1,0:T(8,128)(2,1)} %wd_ref.1, f32[1280]{0:T(1024)} %pg_in.1, f32[1280]{0:T(1024)} %ps_in.1, ...), custom_call_target="tpu_custom_call" | custom-call | tf_op jit(solution)/shard_map/encoder_layer/pallas_call | solution.py:742
  81.7 2.0 %copy.15 = bf16[2,144,1280]{2,1,0:T(8,128)(2,1)} copy(bf16[2,144,1280]{2,1,0:T(8,128)(2,1)} %encoder_layer.1) | data formatting | bytes 1474560

commit v3 on v2

--- a/solution.py
+++ b/solution.py
@@ -32,8 +32,14 @@
         self.length = n * tok
         self.part_heads = self.heads // 2
         self.span = self.part_heads * HEAD_DIM
-        early = self.span // LANES * LANES
-        self.sends = ((0, early), (early, 2 * self.span))
+        total = 2 * self.span
+        self.full = total // LANES
+        self.rest = total % LANES
+        self.fold = 2 if self.rest == LANES // 2 and tok % 16 == 0 else 1
+        rest_rows = tok // self.fold if self.rest else 0
+        self.ctx_rows = self.full * tok + rest_rows
+        early = self.span // LANES * tok
+        self.sends = ((0, early), (early, self.ctx_rows))
         self.part_columns = self.part_heads * 3 * LANES
         columns = self.heads * 3 * HEAD_DIM
         starts = [g * columns for g in range(2 * self.across)]
@@ -103,6 +109,7 @@
     wbuf,
     bpad,
     packed,
+    kept,
     mixed,
     landed,
     ctx,
@@ -345,8 +352,8 @@
     def ctx_copy(part, sp, group, slot):
         low, high = plan.sends[part]
         return remote(
-            mixed.at[sp, :, pl.ds(low, high - low)],
-            landed.at[group, slot, :, pl.ds(low, high - low)],
+            mixed.at[sp, pl.ds(low, high - low)],
+            landed.at[group, slot, pl.ds(low, high - low)],
             c_send.at[part, sp],
             c_recv.at[part, group, slot],
             (pair * 2 + z // images, sp),
@@ -507,9 +514,10 @@
             norm_chunk(zp * across + y, c)
             if c:
                 norm_side(zp, c - 1)
-    pass_first(0)
-    for zp in z_order[1:]:
+    for step, zp in enumerate(z_order[1:]):
         side(zp, chunks - 1)
+        if step == 1:
+            pass_first(0)
         norm_side(zp, chunks - 1)
 
     for k in range(3):
@@ -527,12 +535,36 @@
 
         lax.fori_loop(0, groups, one, 0)
 
-    def attend(part, after):
+    merge = 2 if 2 * block_rows <= 640 else 1
+
+    def put_context(part, rows, sp, store):
+        low, high = plan.sends[part]
+        known = rows
+        start = part * plan.span
+        if part:
+            known = jnp.concatenate([kept[sp], rows], axis=-1)
+            start = 0
+        for tile in range(plan.full):
+            if low <= tile * tok < high:
+                at = tile * LANES - start
+                store(pl.ds(tile * tok, tok), known[:, at : at + LANES])
+        if part and plan.rest:
+            last = known[:, plan.full * LANES :]
+            if plan.fold == 2:
+                last = jnp.concatenate([last[: tok // 2], last[tok // 2 :]], axis=-1)
+            else:
+                last = jnp.concatenate([last, jnp.zeros((tok, LANES - plan.rest), HALF)], axis=-1)
+            store(pl.ds(plan.full * tok, tok // plan.fold), last)
+
+    def attend(part):
         def one(step, carry):
-            near = (step + 1) // 2 % 2
-            far = 1 - step // 2
-            zp = (z + near * (1 - 2 * (z % 2)) + 2 * far) % groups
-            at = pl.ds(pl.multiple_of(zp * block_rows, 16), block_rows)
+            if merge == 2:
+                zp = (z - z % 2 + 2 * (1 - step)) % groups
+            else:
+                near = (step + 1) // 2 % 2
+                far = 1 - step // 2
+                zp = (z + near * (1 - 2 * (z % 2)) + 2 * far) % groups
+            at = pl.ds(pl.multiple_of(zp * block_rows, 16), merge * block_rows)
             outs = []
             for h in range(plan.part_heads):
                 base = h * 3 * LANES
@@ -547,15 +579,22 @@
                 summed = jnp.dot(weights, value_rows, preferred_element_type=jnp.float32)
                 outs.append(summed[:, :HEAD_DIM] / summed[:, HEAD_DIM : HEAD_DIM + 1])
             whole = (jnp.concatenate(outs, axis=-1) if len(outs) > 1 else outs[0]).astype(HALF)
-            for yy in range(across):
+            for yy in range(merge * across):
                 sp = zp * across + yy
-                here = slice(part * plan.span, (part + 1) * plan.span)
-                mixed[sp, :, here] = whole[yy * tok : (yy + 1) * tok]
+                rows = whole[yy * tok : (yy + 1) * tok]
+
+                def to_mixed(run, values):
+                    mixed[sp, run] = values
+
+                put_context(part, rows, sp, to_mixed)
                 own = jnp.logical_and(mine, sp == s)
 
                 @pl.when(own)
                 def _():
-                    landed[group, z % images, :, here] = whole[yy * tok : (yy + 1) * tok]
+                    def to_landed(run, values):
+                        landed[group, z % images, run] = values
+
+                    put_context(part, rows, sp, to_landed)
 
                 if sends_in(part):
 
@@ -563,25 +602,22 @@
                     def _():
                         ctx_copy(part, sp, group, z % images).start()
 
-            for when, action in after:
-
-                @pl.when(step == when)
-                def _():
-                    action()
+                if part == 0:
+                    kept[sp] = rows
 
             return carry
 
-        lax.fori_loop(0, groups, one, 0)
+        lax.fori_loop(0, groups // merge, one, 0)
 
     pad_others(0)
-    project(0)
     for part in range(1, n_parts):
         q_relay(part)
-    attend(0, [])
+    project(0)
+    attend(0)
     pass_first(1)
     pad_others(1)
     project(1)
-    attend(1, [])
+    attend(1)
     pass_first(2)
     pass_first(3)
     pass_first(4)
@@ -593,7 +629,7 @@
         source = (core * images + i) * across + yy
         own = jnp.logical_and(source == s, core == cc)
         low, high = plan.sends[part]
-        slot = landed.at[gg, i, :, pl.ds(low, high - low)]
+        slot = landed.at[gg, i, pl.ds(low, high - low)]
 
         @pl.when(jnp.logical_not(own))
         def _():
@@ -610,7 +646,13 @@
         columns = plan.heads * HEAD_DIM
         for i in range(images):
             for gg in range(2 * across):
-                ctx[i * tok : (i + 1) * tok, gg * columns : (gg + 1) * columns] = landed[gg, i]
+                cut = [landed[gg, i, t * tok : (t + 1) * tok] for t in range(plan.full)]
+                if plan.rest:
+                    last = landed[gg, i, plan.full * tok : plan.ctx_rows]
+                    if plan.fold == 2:
+                        last = jnp.concatenate([last[:, : plan.rest], last[:, plan.rest :]], axis=0)
+                    cut.append(last[:, : plan.rest])
+                ctx[i * tok : (i + 1) * tok, gg * columns : (gg + 1) * columns] = jnp.concatenate(cut, axis=-1)
 
     contexts_in(0)
     pass_second(0)
@@ -621,17 +663,14 @@
     arrived(0)
     row_count = images * tok
 
-    def tile_of(c):
-        return pl.ds(pl.multiple_of(c * 2 * LANES, 2 * LANES), 2 * LANES)
-
-    def out_tile(c, carry):
-        cols = tile_of(c)
+    def project_out(c, carry):
+        cols = pl.ds(pl.multiple_of(c * (plan.width // 2), LANES), plan.width // 2)
         attended = jnp.dot(ctx[...], w_out[:, cols], preferred_element_type=jnp.float32)
-        residual = tok_ref[:, :, cols].astype(jnp.float32).reshape(row_count, 2 * LANES)
+        residual = tok_ref[:, :, cols].astype(jnp.float32).reshape(row_count, plan.width // 2)
         mid[:, cols] = residual + attended + ob_ref[:, cols]
         return carry
 
-    lax.fori_loop(0, plan.width // (2 * LANES), out_tile, 0)
+    lax.fori_loop(0, 2, project_out, 0)
 
     def second_norm(i, carry):
         at = pl.ds(pl.multiple_of(i * NORM_ROWS, 16), NORM_ROWS)
@@ -649,22 +688,30 @@
         for j in range(1, pairs):
             w_s(q, j, second, True).wait_recv()
 
-    ups = [q for q, piece in enumerate(pieces) if piece[0] == 1]
-    downs = [q for q, piece in enumerate(pieces) if piece[0] == 2]
+    def run_columns(first, last, second):
+        k, low, _, along_z = pieces[first]
+        columns = pieces[last][1] + pieces[last][2] - low
+        return piece_columns((k, low, columns, along_z), second)
+
     w_own(1).wait()
     w_so(1, True).wait_recv()
-    for q in ups:
+    for q in (1, 2, 3, 4):
         piece_in(q, False)
-        lift(piece_columns(pieces[q], False))
+    lift(run_columns(1, 1, False))
+    lift(run_columns(2, 3, False))
+    lift(run_columns(4, 4, False))
     pass_first(6)
-    for p, q in enumerate(ups[1:]):
-        pass_second(q)
-        before = ups[p]
-        piece_in(before, True)
-        lift(piece_columns(pieces[before], True))
+    pass_second(2)
+    pass_second(3)
+    piece_in(1, True)
+    piece_in(2, True)
+    lift(run_columns(1, 2, True))
     pass_first(7)
-    piece_in(ups[-1], True)
-    lift(piece_columns(pieces[ups[-1]], True))
+    pass_second(4)
+    piece_in(3, True)
+    lift(run_columns(3, 3, True))
+    piece_in(4, True)
+    lift(run_columns(4, 4, True))
 
     def result_copy(slot, cols):
         return pltpu.make_async_copy(o_ref.at[:, :, cols], o_out.at[:, :, cols], io_sem.at[slot + 1])
@@ -677,53 +724,65 @@
 
     w_own(2).wait()
     w_so(2, True).wait_recv()
-    for p, q in enumerate(downs):
+    lowered_runs = ((5, 5, False), (6, 6, False), (7, 7, False), (5, 5, True), (6, 6, True), (7, 7, True))
+    pass_second(5)
+    for q in (5, 6, 7):
         piece_in(q, False)
-        lower(2 * q, piece_columns(pieces[q], False))
-        pass_second(q)
-    for q in downs:
-        piece_in(q, True)
-        lower(2 * q + 1, piece_columns(pieces[q], True))
-    for second in (False, True):
-        for q in downs:
-            result_copy(2 * q + second, piece_columns(pieces[q], second)).wait()
-
-    for c in range(chunks):
-        for k in range(images):
-
-            @pl.when(core * images + k != z)
+    for slot in range(3):
+        lower(slot, run_columns(*lowered_runs[slot]))
+    pass_second(6)
+    piece_in(5, True)
+    lower(3, run_columns(*lowered_runs[3]))
+    pass_second(7)
+    for slot in (4, 5):
+        piece_in(slot + 2, True)
+        lower(slot, run_columns(*lowered_runs[slot]))
+
+    def results_out():
+        for slot in range(6):
+            result_copy(slot, run_columns(*lowered_runs[slot])).wait()
+
+    results_out()
+
+    def drain():
+        for c in range(chunks):
+            for k in range(images):
+
+                @pl.when(core * images + k != z)
+                def _():
+                    token_z(k, c).wait_send()
+
+            @pl.when(mine)
             def _():
-                token_z(k, c).wait_send()
-
-        @pl.when(mine)
-        def _():
-            for zp in range(groups):
-                for dy in range(1, across):
-                    token_y(zp, dy, c).wait_send()
+                for zp in range(groups):
+                    for dy in range(1, across):
+                        token_y(zp, dy, c).wait_send()
+                for sp in range(n):
+                    token_s(sp, c).wait_send()
+
+        for part in range(n_parts):
+            q_s(part).wait_send()
+            for j in range(1, pairs):
+                for cc in range(2):
+                    q_x(part, j, cc).wait_send()
+                    q_z(part, j, cc).wait_send()
+        for k in range(3):
+            w_so(k).wait_send()
+        for q in range(len(pieces)):
+            for j in range(1, pairs):
+                w_x(q, j).wait_send()
+                w_p(q, j).wait_send()
+                w_s(q, j, False).wait_send()
+                w_s(q, j, True).wait_send()
+        for part in range(2):
             for sp in range(n):
-                token_s(sp, c).wait_send()
-
-    for part in range(n_parts):
-        q_s(part).wait_send()
-        for j in range(1, pairs):
-            for cc in range(2):
-                q_x(part, j, cc).wait_send()
-                q_z(part, j, cc).wait_send()
-    for k in range(3):
-        w_so(k).wait_send()
-    for q in range(len(pieces)):
-        for j in range(1, pairs):
-            w_x(q, j).wait_send()
-            w_p(q, j).wait_send()
-            w_s(q, j, False).wait_send()
-            w_s(q, j, True).wait_send()
-    for part in range(2):
-        for sp in range(n):
-
-            @pl.when(jnp.logical_not(jnp.logical_and(mine, sp == s)))
-            def _():
-                if sends_in(part):
-                    ctx_copy(part, sp, group, z % images).wait_send()
+
+                @pl.when(jnp.logical_not(jnp.logical_and(mine, sp == s)))
+                def _():
+                    if sends_in(part):
+                        ctx_copy(part, sp, group, z % images).wait_send()
+
+    drain()
 
 
 def shards(n, n_dp, tokens, pre_gain, pre_shift, w_qkv, qkv_bias, w_out, out_bias, mlp_gain, mlp_shift,
@@ -756,8 +815,9 @@
             pltpu.VMEM((2, width, plan.part_columns), HALF),
             pltpu.VMEM((2, 1, plan.part_columns), jnp.float32),
             pltpu.VMEM((2, plan.length, plan.part_columns), HALF),
-            pltpu.VMEM((n, tok, 2 * plan.span), HALF),
-            pltpu.VMEM((2 * across, images, tok, 2 * plan.span), HALF),
+            pltpu.VMEM((n, tok, plan.span), HALF),
+            pltpu.VMEM((n, plan.ctx_rows, LANES), HALF),
+            pltpu.VMEM((2 * across, images, plan.ctx_rows, LANES), HALF),
             pltpu.VMEM((rows, width), HALF),
             pltpu.VMEM((rows, width), jnp.float32),
             pltpu.VMEM((rows, hidden), HALF),

time: 84.3 us -> 79.8 us (0.947)
  Pallas kernels: 81.7 us -> 77.6 us
    pallas_call x1, Pallas kernels: 81.7 us -> 77.6 us  [shards(): pl.pallas_call(functools.partial(layer_kernel, plan), out_shape=jax.Shape...]
where the time goes in v3:
time: 79.8 us; the launch traced here: 79.6 us
  Pallas kernels  77.6 us (97%)
  local copies, waits for them, and re-layouts  2.03 us (3%)
    pallas_call x1, Pallas kernels, shards(): pl.pallas_call(functools.partial(layer_kernel, plan), out_shape=jax.Shape...  77.6 us
    unnamed x1, local copies, waits for them, and re-layouts  2.03 us

profile of v3, /device:TPU:1, one launch (start us, length us, event | category | flops | bytes accessed | tf_op | source)
XLA Modules:
  0.0 79.6 jit_solution(4069959111676792893)
XLA Ops:
  0.0 77.6 %encoder_layer.1 = bf16[2,144,1280]{2,1,0:T(8,128)(2,1)} custom-call(bf16[2,144,1280]{2,1,0:T(8,128)(2,1)} %tok_in.1, bf16[320,3840]{1,0:T(8,128)(2,1)} %wq_ref.1, bf16[320,1280]{1,0:T(8,128)(2,1)} %wo_ref.1, bf16[320,2560]{1,0:T(8,128)(2,1)} %wu_ref.1, bf16[640,1280]{1,0:T(8,128)(2,1)} %wd_ref.1, f32[1280]{0:T(1024)} %pg_in.1, f32[1280]{0:T(1024)} %ps_in.1, ...), custom_call_target="tpu_custom_call" | custom-call | tf_op jit(solution)/shard_map/encoder_layer/pallas_call | solution.py:801
  77.6 2.0 %copy.15 = bf16[2,144,1280]{2,1,0:T(8,128)(2,1)} copy(bf16[2,144,1280]{2,1,0:T(8,128)(2,1)} %encoder_layer.1) | data formatting | bytes 1474560
